TPU v7x, 32 devices: a whole 2x2x4 slice. The times are simulated.
32 devices in a mesh: mem: 8 (over z, x), blk: 4 (over y, core).
Axes of the slice: x: 2, y: 2, z: 4, core: 2. Of those that a mesh axis runs over, the one named last changes fastest.
Arguments:
- ensemble: bfloat16 [128, 131072], P('mem', 'blk'), may hold values from -6 to 6
- obs_cell: int32 [4, 64, 256], P('blk', 'mem'), may hold values from 0 to 511
- obs_count: int32 [4, 64], P('blk', 'mem'), may hold values from 1 to 256, 10240 in all within a row
- obs_value: float32 [4, 64, 256], P('blk', 'mem'), may hold values from -6 to 6
- obs_rinv: float32 [4, 64, 256], P('blk', 'mem'), may hold values from 0.05 to 0.5
Outputs:
- increments: bfloat16 [128, 131072], P('mem', 'blk')
Inputs may be any that keep to these rules, and one draw needn't show every extreme that they name: `obs_cell`: slots at or past the block's count are unused. `obs_count`: the counts of one band sum to 10240, and some block holds exactly 256.
All inputs are finite; a program needn't handle non-finite values. Where the computation divides by a largest or mean magnitude, that divisor is 1e-20 or more.
Results may differ from a plain program's by a relative error of at most 0.0051.
Values may be sent and summed in bfloat16 or wider, within the bound.
A program may use at most 64 MiB of HBM per device.

v0:
```python
import functools

import jax
import jax.numpy as jnp
from jax import lax
from jax.experimental import pallas as pl
from jax.experimental.pallas import tpu as pltpu
from jax.sharding import PartitionSpec as P

NS_ITERS = 4


localize = 0.5
inflation = 1.1

MESH = pl.DeviceIdType.MESH
WINDOW = 3
F32 = jnp.float32
BF16 = jnp.bfloat16


def halves(x):
    high = x.astype(BF16)
    return high, (x - high.astype(F32)).astype(BF16)


def as_left(x):
    return jnp.concatenate(halves(x), axis=1)


def as_right(x):
    wide = jnp.concatenate(halves(x), axis=1)
    return jnp.concatenate([wide, wide], axis=0)


def mm(left, right):
    both = jnp.dot(left, right, preferred_element_type=F32)
    size = both.shape[1] // 2
    return both[:, :size] + both[:, size:]


def observed_rows(members, selector, values, root):
    ensemble_size = members.shape[0]
    sampled = jnp.dot(members, selector, preferred_element_type=F32)
    obs_mean = jnp.sum(sampled, axis=0, keepdims=True) * (1.0 / ensemble_size)
    upper = ((sampled - obs_mean) * root).astype(BF16)
    lower = root * (values - obs_mean)
    place = lax.broadcasted_iota(jnp.int32, (16, lower.shape[1]), 0)
    lower = jnp.where(place == 0, jnp.broadcast_to(lower, place.shape), 0.0).astype(BF16)
    return jnp.concatenate([upper, lower], axis=0)


def increments_of(localized, members):
    ensemble_size = members.shape[0]
    row = lax.broadcasted_iota(jnp.int32, (ensemble_size, ensemble_size), 0)
    column = lax.broadcasted_iota(jnp.int32, (ensemble_size, ensemble_size), 1)
    identity = (row == column).astype(F32)
    system = (ensemble_size - 1) / inflation * identity + localized[:ensemble_size]
    bound_norm = jnp.max(
        jnp.sum(jnp.abs(system), axis=0, keepdims=True), axis=1, keepdims=True
    )
    approx_y = system / bound_norm
    update = 1.5 * identity - 0.5 * approx_y
    approx_z = update
    for iteration in range(1, NS_ITERS):
        approx_y = mm(as_left(approx_y), as_right(update))
        left_z = as_left(approx_z)
        update = 1.5 * identity - 0.5 * mm(left_z, as_right(approx_y))
        approx_z = mm(left_z, as_right(update))
    root_inv = approx_z / jnp.sqrt(bound_norm)
    right_r = as_right(root_inv)
    inner = mm(as_left(localized[ensemble_size:]), right_r)
    mean_weights = mm(as_left(inner), right_r)[0:1]
    mixing = jnp.sqrt(F32(ensemble_size - 1)) * root_inv + mean_weights - identity
    high, low = halves(mixing)
    row_sum = jnp.sum(high.astype(F32) + low.astype(F32), axis=1, keepdims=True)
    average = jnp.sum(members.astype(F32), axis=0, keepdims=True) * (1.0 / ensemble_size)
    total = jnp.dot(
        jnp.concatenate([high, low], axis=1),
        jnp.concatenate([members, members], axis=0),
        preferred_element_type=F32,
    )
    return (total - row_sum * average).astype(BF16)


def kernel(
    groups,
    ens_hbm,
    cell_hbm,
    count_hbm,
    value_hbm,
    rinv_hbm,
    out,
    arrived,
    rows,
    gram,
    edge,
    far_edge,
    selector,
    stage,
    weight,
    ens,
    cell,
    count,
    value,
    rinv,
    load_sem,
    own_sem,
    fwd_send,
    fwd_recv,
    ret_send,
    ret_recv,
    halo_send,
    halo_recv,
):
    me = lax.axis_index("mem")
    blocks, _, width = arrived.shape
    local = ens.shape[0]
    slots = cell.shape[1]
    size = groups * local

    barrier = pltpu.get_barrier_semaphore()
    for step in range(1, groups):
        pl.semaphore_signal(
            barrier, inc=1, device_id={"mem": lax.rem(me + step, groups)}, device_id_type=MESH
        )

    loads = [
        pltpu.make_async_copy(source, target, load_sem.at[i])
        for i, (source, target) in enumerate(
            (
                (ens_hbm, ens),
                (cell_hbm, cell),
                (count_hbm, count),
                (value_hbm, value),
                (rinv_hbm, rinv),
            )
        )
    ]
    for load in loads:
        load.start()
    loads[0].wait()
    pl.semaphore_wait(barrier, groups - 1)

    def columns(owner, b):
        start = pl.multiple_of((owner * blocks + b) * width, width)
        return pl.ds(start, width)

    def members_of(owner):
        return pl.ds(pl.multiple_of(owner * local, local), local)

    def send_block(i):
        b = lax.rem(i + blocks - 1, blocks)
        for step in range(1, groups):
            peer = lax.rem(me + step, groups)
            pltpu.make_async_remote_copy(
                src_ref=ens.at[:, columns(peer, b)],
                dst_ref=arrived.at[b, members_of(me), :],
                send_sem=fwd_send,
                recv_sem=fwd_recv.at[b],
                device_id={"mem": peer},
                device_id_type=MESH,
            ).start()
        pltpu.make_async_copy(
            ens.at[:, columns(me, b)], arrived.at[b, members_of(me), :], fwd_recv.at[b]
        ).start()

    for i in range(min(WINDOW, blocks)):
        send_block(i)

    def send_ahead(i):
        @pl.when(i + WINDOW < blocks)
        def _():
            send_block(i + WINDOW)

    for load in loads[1:]:
        load.wait()
    weight[...] = jnp.sqrt(rinv[...])

    @pl.loop(0, blocks)
    def _(b):
        positions = lax.broadcasted_iota(jnp.int32, (width, slots), 0)
        selector[b] = jnp.where(positions == cell[pl.ds(b, 1), :], 1.0, 0.0).astype(BF16)

    def form_gram(slot):
        held = rows[slot]
        gram[slot] = lax.dot_general(
            held, held[:size], (((1,), (1,)), ((), ())), preferred_element_type=F32
        )

    def take_block(b):
        pltpu.make_async_copy(arrived.at[b], arrived.at[b], fwd_recv.at[b]).wait()
        send_ahead(lax.rem(jnp.int32(b) + 1, blocks))
        alive = lax.broadcasted_iota(jnp.int32, (1, slots), 1) < count[0, b]
        root = jnp.where(alive, weight[pl.ds(b, 1), :], 0.0)
        rows[b + 1] = observed_rows(arrived[b], selector[b], value[pl.ds(b, 1), :], root)

    def give_block(b):
        localized = gram[b + 1] + localize * (gram[b] + gram[b + 2])
        pair = b // 2
        part = pl.ds(pl.multiple_of((b % 2) * width, width), width)
        stage[pair, :, part] = increments_of(localized, arrived[b])

        @pl.when(b % 2 == 1)
        def _():
            both = pl.ds(pl.multiple_of((me * blocks + b - 1) * width, width), 2 * width)
            for step in range(1, groups):
                peer = lax.rem(me + step, groups)
                pltpu.make_async_remote_copy(
                    src_ref=stage.at[pair, members_of(peer), :],
                    dst_ref=out.at[:, both],
                    send_sem=ret_send,
                    recv_sem=ret_recv,
                    device_id={"mem": peer},
                    device_id_type=MESH,
                ).start()
            pltpu.make_async_copy(
                stage.at[pair, members_of(me), :], out.at[:, both], own_sem
            ).start()

    def halo(slot, peer, which):
        edge[which] = gram[slot].astype(BF16)
        return pltpu.make_async_remote_copy(
            src_ref=edge.at[which],
            dst_ref=far_edge.at[which],
            send_sem=halo_send.at[which],
            recv_sem=halo_recv.at[which],
            device_id={"mem": peer},
            device_id_type=MESH,
        )

    take_block(blocks - 1)
    form_gram(blocks)
    upward = halo(blocks, lax.rem(me + 1, groups), 0)
    upward.start()
    take_block(0)
    form_gram(1)
    downward = halo(1, lax.rem(me + groups - 1, groups), 1)
    downward.start()
    take_block(1)
    form_gram(2)
    upward.wait_recv()
    gram[0] = far_edge[0].astype(F32)
    give_block(jnp.int32(0))

    @pl.loop(2, blocks - 1)
    def _(b):
        take_block(b)
        form_gram(b + 1)
        give_block(b - 1)

    downward.wait_recv()
    gram[blocks + 1] = far_edge[1].astype(F32)

    @pl.loop(blocks - 2, blocks)
    def _(b):
        give_block(b)

    upward.wait_send()
    downward.wait_send()
    share = blocks * width
    afar = pl.ds(0, (groups - 1) * share)
    pltpu.make_async_copy(ens.at[:, afar], ens.at[:, afar], fwd_send).wait()
    pltpu.make_async_copy(out.at[:, afar], out.at[:, afar], ret_send).wait()
    pltpu.make_async_copy(out.at[:, afar], out.at[:, afar], ret_recv).wait()
    near = pl.ds(0, share)
    pltpu.make_async_copy(out.at[:, near], out.at[:, near], own_sem).wait()


def fused(ensemble, obs_cell, obs_count, obs_value, obs_rinv):
    groups = lax.axis_size("mem")
    local, cells = ensemble.shape
    blocks, slots = obs_cell.shape[1:]
    width = cells // (groups * blocks)
    size = groups * local
    whole = pl.BlockSpec(memory_space=pltpu.VMEM)
    return pl.pallas_call(
        functools.partial(kernel, groups),
        out_shape=pltpu.VMEM(ensemble.shape, BF16),
        in_specs=[pl.BlockSpec(memory_space=pl.ANY)] * 5,
        out_specs=whole,
        scratch_shapes=[
            pltpu.VMEM((blocks, size, width), BF16),
            pltpu.VMEM((blocks + 2, size + 16, slots), BF16),
            pltpu.VMEM((blocks + 2, size + 16, size), F32),
            pltpu.VMEM((2, size + 16, size), BF16),
            pltpu.VMEM((2, size + 16, size), BF16),
            pltpu.VMEM((blocks, width, slots), BF16),
            pltpu.VMEM((blocks // 2, size, 2 * width), BF16),
            pltpu.VMEM((blocks, slots), F32),
            pltpu.VMEM(ensemble.shape, BF16),
            pltpu.VMEM((blocks, slots), jnp.int32),
            pltpu.SMEM(obs_count.shape, jnp.int32),
            pltpu.VMEM((blocks, slots), F32),
            pltpu.VMEM((blocks, slots), F32),
            pltpu.SemaphoreType.DMA((5,)),
            pltpu.SemaphoreType.DMA,
            pltpu.SemaphoreType.DMA,
            pltpu.SemaphoreType.DMA((blocks,)),
            pltpu.SemaphoreType.DMA,
            pltpu.SemaphoreType.DMA,
            pltpu.SemaphoreType.DMA((2,)),
            pltpu.SemaphoreType.DMA((2,)),
        ],
        compiler_params=pltpu.CompilerParams(collective_id=0, has_side_effects=True),
        name="letkf",
    )(ensemble, obs_cell[0], obs_count, obs_value[0], obs_rinv[0])


def with_halo(block, sides, width):
    for axis, dim in sides:
        count = lax.axis_size(axis)
        forward = [(i, i + 1) for i in range(count - 1)]
        forward.append((count - 1, 0))
        backward = [(target, source) for source, target in forward]
        low = lax.ppermute(
            lax.slice_in_dim(block, block.shape[dim] - width, None, axis=dim), axis, forward
        )
        high = lax.ppermute(lax.slice_in_dim(block, 0, width, axis=dim), axis, backward)
        block = jnp.concatenate([low, block, high], axis=dim)
    return block


def center_blocks(members):
    values = jnp.transpose(members.astype(jnp.float32), (1, 0, 2))
    average = jnp.mean(values, axis=1)
    return (values - average[:, None, :], average)


def observe(deviation, average, cell_ids, live_counts, obs_values, inv_var):
    cell_width = deviation.shape[2]
    positions = lax.broadcasted_iota(jnp.int32, cell_ids.shape + (cell_width,), 2)
    selector = (positions == cell_ids[:, :, None]).astype(jnp.float32)
    sampled = jnp.einsum("bkc,boc->bko", deviation, selector, precision=lax.Precision.HIGHEST)
    obs_mean = jnp.einsum("bc,boc->bo", average, selector, precision=lax.Precision.HIGHEST)
    slots = lax.broadcasted_iota(jnp.int32, cell_ids.shape, 1)
    live = (slots < live_counts[:, None]).astype(jnp.float32)
    weight_root = live * jnp.sqrt(inv_var)
    upper = sampled * weight_root[:, None, :]
    lower = (weight_root * (obs_values - obs_mean))[:, None, :]
    return jnp.concatenate([upper, lower], axis=1).astype(jnp.bfloat16)


def gram_of(obs_rows):
    return jnp.einsum("bko,bjo->bkj", obs_rows, obs_rows, preferred_element_type=jnp.float32)


def batch_mm(left, right):
    return jnp.einsum("bij,bjk->bik", left, right, precision=lax.Precision.HIGHEST)


def transform_apply(localized, deviation):
    ensemble_size = deviation.shape[1]
    identity = jnp.eye(ensemble_size, dtype=jnp.float32)
    system = (ensemble_size - 1) / inflation * identity + localized[
        :, :ensemble_size, :ensemble_size
    ]
    forcing = localized[:, :ensemble_size, ensemble_size]
    bound_norm = jnp.max(jnp.sum(jnp.abs(system), axis=2), axis=1)
    approx_y = system / bound_norm[:, None, None]
    approx_z = jnp.broadcast_to(identity, system.shape)
    for iteration in range(NS_ITERS):
        update = 1.5 * identity - 0.5 * batch_mm(approx_z, approx_y)
        approx_y = batch_mm(approx_y, update)
        approx_z = batch_mm(update, approx_z)
    root_inv = approx_z / jnp.sqrt(bound_norm)[:, None, None]
    inner = jnp.einsum("bij,bj->bi", root_inv, forcing, precision=lax.Precision.HIGHEST)
    mean_weights = jnp.einsum("bij,bj->bi", root_inv, inner, precision=lax.Precision.HIGHEST)
    mixing = (
        jnp.sqrt(jnp.float32(ensemble_size - 1)) * root_inv + mean_weights[:, :, None] - identity
    )
    increment = jnp.einsum("bjc,bjk->kbc", deviation, mixing, precision=lax.Precision.HIGHEST)
    return increment.astype(jnp.bfloat16)


def on_device(ensemble, obs_cell, obs_count, obs_value, obs_rinv):
    groups = lax.axis_size("mem")
    local_members = ensemble.shape[0]
    blocks = obs_cell.shape[1]
    cell_width = ensemble.shape[1] // (groups * blocks)
    pieces = ensemble.reshape(local_members, groups, blocks, cell_width)
    arrived = lax.all_to_all(pieces, "mem", split_axis=1, concat_axis=0, tiled=True)
    deviation, average = center_blocks(arrived[:, 0])
    obs_rows = observe(deviation, average, obs_cell[0], obs_count[0], obs_value[0], obs_rinv[0])
    padded_rows = with_halo(obs_rows, (("mem", 0),), 1)
    padded = gram_of(padded_rows)
    localized = padded[1:-1] + localize * (padded[:-2] + padded[2:])
    increment = transform_apply(localized, deviation)
    ensemble_size = increment.shape[0]
    outgoing = increment.reshape(ensemble_size, 1, blocks * cell_width)
    returned = lax.all_to_all(outgoing, "mem", split_axis=0, concat_axis=1, tiled=True)
    return returned.reshape(local_members, groups * blocks * cell_width)


def by_shape(ensemble, *observations):
    groups = lax.axis_size("mem")
    local, cells = ensemble.shape
    blocks, slots = observations[0].shape[1:]
    width = cells // (groups * blocks)
    aligned = local % 16 == 0 and width % 128 == 0 and slots % 128 == 0
    aligned = aligned and (groups * local) % 128 == 0 and groups > 1 and blocks > 2 and blocks % 2 == 0
    return (fused if aligned else on_device)(ensemble, *observations)


def solution(mesh):
    placed = (
        P("mem", "blk"),
        P("blk", "mem", None),
        P("blk", "mem"),
        P("blk", "mem", None),
        P("blk", "mem", None),
    )
    return jax.shard_map(
        by_shape, mesh=mesh, in_specs=placed, out_specs=P("mem", "blk"), check_vma=False
    )
```

profile of v0, /device:TPU:0, one launch (start us, length us, event | category | flops | bytes accessed | tf_op | source)
XLA Modules:
  0.0 52.7 jit_solution(2781497119645629781)
XLA Ops:
  0.0 51.7 %letkf.1 = bf16[16,32768]{1,0:T(8,128)(2,1)S(1)} custom-call(bf16[16,32768]{1,0:T(8,128)(2,1)} %ens_hbm.1, s32[8,256]{1,0:T(8,128)} %bitcast.3, s32[1,8]{1,0:T(1,128)} %count_hbm.1, f32[8,256]{1,0:T(8,128)} %bitcast.4, f32[8,256]{1,0:T(8,128)} %bitcast.5), custom_call_target="tpu_custom_call" | custom-call | tf_op jit(solution)/shard_map/letkf/pallas_call | solution.py:277
  51.7 1.0 %copy.7 = bf16[16,32768]{1,0:T(8,128)(2,1)} copy(bf16[16,32768]{1,0:T(8,128)(2,1)S(1)} %letkf.1) | data formatting | bytes 2097152
where the time goes:
time: 52.8 us; the launch traced here: 52.7 us
  Pallas kernels  51.7 us (98%)
  local copies, waits for them, and re-layouts  0.97 us (2%)
    pallas_call x1, Pallas kernels, fused(): pl.pallas_call(functools.partial(kernel, groups), out_shape=pltpu.VMEM(en...  51.7 us

commit v1 on v0

--- a/solution.py
+++ b/solution.py
@@ -14,7 +14,8 @@
 inflation = 1.1
 
 MESH = pl.DeviceIdType.MESH
-WINDOW = 3
+CHUNK = 1
+HELD_BACK = 2
 F32 = jnp.float32
 BF16 = jnp.bfloat16
 
@@ -51,36 +52,47 @@
 
 
 def increments_of(localized, members):
-    ensemble_size = members.shape[0]
+    ensemble_size = members[0].shape[0]
     row = lax.broadcasted_iota(jnp.int32, (ensemble_size, ensemble_size), 0)
     column = lax.broadcasted_iota(jnp.int32, (ensemble_size, ensemble_size), 1)
     identity = (row == column).astype(F32)
-    system = (ensemble_size - 1) / inflation * identity + localized[:ensemble_size]
-    bound_norm = jnp.max(
-        jnp.sum(jnp.abs(system), axis=0, keepdims=True), axis=1, keepdims=True
-    )
-    approx_y = system / bound_norm
-    update = 1.5 * identity - 0.5 * approx_y
+    system = [
+        (ensemble_size - 1) / inflation * identity + part[:ensemble_size] for part in localized
+    ]
+    bound_norm = [
+        jnp.max(jnp.sum(jnp.abs(part), axis=0, keepdims=True), axis=1, keepdims=True)
+        for part in system
+    ]
+    approx_y = [part / norm for part, norm in zip(system, bound_norm)]
+    update = [1.5 * identity - 0.5 * part for part in approx_y]
     approx_z = update
     for iteration in range(1, NS_ITERS):
-        approx_y = mm(as_left(approx_y), as_right(update))
-        left_z = as_left(approx_z)
-        update = 1.5 * identity - 0.5 * mm(left_z, as_right(approx_y))
-        approx_z = mm(left_z, as_right(update))
-    root_inv = approx_z / jnp.sqrt(bound_norm)
-    right_r = as_right(root_inv)
-    inner = mm(as_left(localized[ensemble_size:]), right_r)
-    mean_weights = mm(as_left(inner), right_r)[0:1]
-    mixing = jnp.sqrt(F32(ensemble_size - 1)) * root_inv + mean_weights - identity
-    high, low = halves(mixing)
-    row_sum = jnp.sum(high.astype(F32) + low.astype(F32), axis=1, keepdims=True)
-    average = jnp.sum(members.astype(F32), axis=0, keepdims=True) * (1.0 / ensemble_size)
-    total = jnp.dot(
-        jnp.concatenate([high, low], axis=1),
-        jnp.concatenate([members, members], axis=0),
-        preferred_element_type=F32,
-    )
-    return (total - row_sum * average).astype(BF16)
+        approx_y = [mm(as_left(y), as_right(u)) for y, u in zip(approx_y, update)]
+        left_z = [as_left(z) for z in approx_z]
+        update = [
+            1.5 * identity - 0.5 * mm(z, as_right(y)) for z, y in zip(left_z, approx_y)
+        ]
+        approx_z = [mm(z, as_right(u)) for z, u in zip(left_z, update)]
+    root_inv = [z / jnp.sqrt(norm) for z, norm in zip(approx_z, bound_norm)]
+    right_r = [as_right(part) for part in root_inv]
+    inner = [mm(as_left(part[ensemble_size:]), r) for part, r in zip(localized, right_r)]
+    mean_weights = [mm(as_left(part), r)[0:1] for part, r in zip(inner, right_r)]
+    mixing = [
+        jnp.sqrt(F32(ensemble_size - 1)) * part + weights - identity
+        for part, weights in zip(root_inv, mean_weights)
+    ]
+    results = []
+    for mixed, block in zip(mixing, members):
+        high, low = halves(mixed)
+        row_sum = jnp.sum(high.astype(F32) + low.astype(F32), axis=1, keepdims=True)
+        average = jnp.sum(block.astype(F32), axis=0, keepdims=True) * (1.0 / ensemble_size)
+        total = jnp.dot(
+            jnp.concatenate([high, low], axis=1),
+            jnp.concatenate([block, block], axis=0),
+            preferred_element_type=F32,
+        )
+        results.append((total - row_sum * average).astype(BF16))
+    return results
 
 
 def kernel(
@@ -99,7 +111,6 @@
     selector,
     stage,
     weight,
-    ens,
     cell,
     count,
     value,
@@ -115,7 +126,7 @@
 ):
     me = lax.axis_index("mem")
     blocks, _, width = arrived.shape
-    local = ens.shape[0]
+    local = ens_hbm.shape[0]
     slots = cell.shape[1]
     size = groups * local
 
@@ -128,18 +139,11 @@
     loads = [
         pltpu.make_async_copy(source, target, load_sem.at[i])
         for i, (source, target) in enumerate(
-            (
-                (ens_hbm, ens),
-                (cell_hbm, cell),
-                (count_hbm, count),
-                (value_hbm, value),
-                (rinv_hbm, rinv),
-            )
+            ((cell_hbm, cell), (count_hbm, count), (value_hbm, value), (rinv_hbm, rinv))
         )
     ]
     for load in loads:
         load.start()
-    loads[0].wait()
     pl.semaphore_wait(barrier, groups - 1)
 
     def columns(owner, b):
@@ -149,31 +153,25 @@
     def members_of(owner):
         return pl.ds(pl.multiple_of(owner * local, local), local)
 
-    def send_block(i):
-        b = lax.rem(i + blocks - 1, blocks)
+    order = [blocks - 1, *range(blocks - 1)]
+    for first in range(0, blocks, CHUNK):
         for step in range(1, groups):
             peer = lax.rem(me + step, groups)
-            pltpu.make_async_remote_copy(
-                src_ref=ens.at[:, columns(peer, b)],
-                dst_ref=arrived.at[b, members_of(me), :],
-                send_sem=fwd_send,
-                recv_sem=fwd_recv.at[b],
-                device_id={"mem": peer},
-                device_id_type=MESH,
-            ).start()
+            for b in order[first : first + CHUNK]:
+                pltpu.make_async_remote_copy(
+                    src_ref=ens_hbm.at[:, columns(peer, b)],
+                    dst_ref=arrived.at[b, members_of(me), :],
+                    send_sem=fwd_send,
+                    recv_sem=fwd_recv.at[b],
+                    device_id={"mem": peer},
+                    device_id_type=MESH,
+                ).start()
+    for b in order:
         pltpu.make_async_copy(
-            ens.at[:, columns(me, b)], arrived.at[b, members_of(me), :], fwd_recv.at[b]
+            ens_hbm.at[:, columns(me, b)], arrived.at[b, members_of(me), :], fwd_recv.at[b]
         ).start()
 
-    for i in range(min(WINDOW, blocks)):
-        send_block(i)
-
-    def send_ahead(i):
-        @pl.when(i + WINDOW < blocks)
-        def _():
-            send_block(i + WINDOW)
-
-    for load in loads[1:]:
+    for load in loads:
         load.wait()
     weight[...] = jnp.sqrt(rinv[...])
 
@@ -182,40 +180,37 @@
         positions = lax.broadcasted_iota(jnp.int32, (width, slots), 0)
         selector[b] = jnp.where(positions == cell[pl.ds(b, 1), :], 1.0, 0.0).astype(BF16)
 
-    def form_gram(slot):
-        held = rows[slot]
-        gram[slot] = lax.dot_general(
-            held, held[:size], (((1,), (1,)), ((), ())), preferred_element_type=F32
-        )
-
     def take_block(b):
         pltpu.make_async_copy(arrived.at[b], arrived.at[b], fwd_recv.at[b]).wait()
-        send_ahead(lax.rem(jnp.int32(b) + 1, blocks))
         alive = lax.broadcasted_iota(jnp.int32, (1, slots), 1) < count[0, b]
         root = jnp.where(alive, weight[pl.ds(b, 1), :], 0.0)
-        rows[b + 1] = observed_rows(arrived[b], selector[b], value[pl.ds(b, 1), :], root)
-
-    def give_block(b):
-        localized = gram[b + 1] + localize * (gram[b] + gram[b + 2])
-        pair = b // 2
-        part = pl.ds(pl.multiple_of((b % 2) * width, width), width)
-        stage[pair, :, part] = increments_of(localized, arrived[b])
-
-        @pl.when(b % 2 == 1)
-        def _():
-            both = pl.ds(pl.multiple_of((me * blocks + b - 1) * width, width), 2 * width)
-            for step in range(1, groups):
-                peer = lax.rem(me + step, groups)
+        held = observed_rows(arrived[b], selector[b], value[pl.ds(b, 1), :], root)
+        rows[b] = held
+        gram[b + 1] = lax.dot_general(
+            held, held[:size], (((1,), (1,)), ((), ())), preferred_element_type=F32
+        )
+
+    def solve(pair):
+        localized = [gram[b + 1] + localize * (gram[b] + gram[b + 2]) for b in pair]
+        results = increments_of(localized, [arrived[b] for b in pair])
+        for b, result in zip(pair, results):
+            stage[b] = result
+
+    def give_back(group):
+        for step in range(1, groups):
+            peer = lax.rem(me + step, groups)
+            for b in group:
                 pltpu.make_async_remote_copy(
-                    src_ref=stage.at[pair, members_of(peer), :],
-                    dst_ref=out.at[:, both],
+                    src_ref=stage.at[b, members_of(peer), :],
+                    dst_ref=out.at[:, columns(me, b)],
                     send_sem=ret_send,
                     recv_sem=ret_recv,
                     device_id={"mem": peer},
                     device_id_type=MESH,
                 ).start()
+        for b in group:
             pltpu.make_async_copy(
-                stage.at[pair, members_of(me), :], out.at[:, both], own_sem
+                stage.at[b, members_of(me), :], out.at[:, columns(me, b)], own_sem
             ).start()
 
     def halo(slot, peer, which):
@@ -230,37 +225,48 @@
         )
 
     take_block(blocks - 1)
-    form_gram(blocks)
     upward = halo(blocks, lax.rem(me + 1, groups), 0)
     upward.start()
     take_block(0)
-    form_gram(1)
     downward = halo(1, lax.rem(me + groups - 1, groups), 1)
     downward.start()
+
     take_block(1)
-    form_gram(2)
-    upward.wait_recv()
-    gram[0] = far_edge[0].astype(F32)
-    give_block(jnp.int32(0))
-
-    @pl.loop(2, blocks - 1)
-    def _(b):
-        take_block(b)
-        form_gram(b + 1)
-        give_block(b - 1)
-
-    downward.wait_recv()
-    gram[blocks + 1] = far_edge[1].astype(F32)
-
-    @pl.loop(blocks - 2, blocks)
-    def _(b):
-        give_block(b)
+    pairs = blocks // 2
+
+    @pl.loop(0, pairs)
+    def _(turn):
+        b = 2 * turn + 1
+
+        @pl.when(turn < pairs - 1)
+        def _():
+            @pl.loop(b + 1, jnp.minimum(b + 3, blocks - 1))
+            def _(later):
+                take_block(later)
+
+        @pl.when(turn == pairs - 1)
+        def _():
+            upward.wait_recv()
+            gram[0] = far_edge[0].astype(F32)
+            downward.wait_recv()
+            gram[blocks + 1] = far_edge[1].astype(F32)
+
+        final = turn == pairs - 1
+        solve([jnp.where(final, 0, b), jnp.where(final, blocks - 1, b + 1)])
+
+        for i in range(pairs - HELD_BACK):
+            @pl.when(turn == i)
+            def _():
+                give_back([2 * i + 1, 2 * i + 2])
+
+    held_back = [*range(2 * (pairs - HELD_BACK) + 1, blocks), 0]
+    give_back(held_back)
 
     upward.wait_send()
     downward.wait_send()
     share = blocks * width
     afar = pl.ds(0, (groups - 1) * share)
-    pltpu.make_async_copy(ens.at[:, afar], ens.at[:, afar], fwd_send).wait()
+    pltpu.make_async_copy(out.at[:, afar], out.at[:, afar], fwd_send).wait()
     pltpu.make_async_copy(out.at[:, afar], out.at[:, afar], ret_send).wait()
     pltpu.make_async_copy(out.at[:, afar], out.at[:, afar], ret_recv).wait()
     near = pl.ds(0, share)
@@ -281,19 +287,18 @@
         out_specs=whole,
         scratch_shapes=[
             pltpu.VMEM((blocks, size, width), BF16),
-            pltpu.VMEM((blocks + 2, size + 16, slots), BF16),
+            pltpu.VMEM((blocks, size + 16, slots), BF16),
             pltpu.VMEM((blocks + 2, size + 16, size), F32),
             pltpu.VMEM((2, size + 16, size), BF16),
             pltpu.VMEM((2, size + 16, size), BF16),
             pltpu.VMEM((blocks, width, slots), BF16),
-            pltpu.VMEM((blocks // 2, size, 2 * width), BF16),
+            pltpu.VMEM((blocks, size, width), BF16),
             pltpu.VMEM((blocks, slots), F32),
-            pltpu.VMEM(ensemble.shape, BF16),
             pltpu.VMEM((blocks, slots), jnp.int32),
             pltpu.SMEM(obs_count.shape, jnp.int32),
             pltpu.VMEM((blocks, slots), F32),
             pltpu.VMEM((blocks, slots), F32),
-            pltpu.SemaphoreType.DMA((5,)),
+            pltpu.SemaphoreType.DMA((4,)),
             pltpu.SemaphoreType.DMA,
             pltpu.SemaphoreType.DMA,
             pltpu.SemaphoreType.DMA((blocks,)),

time: 52.8 us -> 51.7 us (0.979); the launches traced: 52.7 us -> 51 us
  Pallas kernels: 51.7 us -> 50 us
    pallas_call x1, Pallas kernels: 51.7 us -> 50 us  [fused(): pl.pallas_call(functools.partial(kernel, groups), out_shape=pltpu.VMEM(en...]
where the time goes in v1:
time: 51.7 us; the launch traced here: 51 us
  Pallas kernels  50 us (97%)
  local copies, waits for them, and re-layouts  0.97 us (2%)
    pallas_call x1, Pallas kernels, fused(): pl.pallas_call(functools.partial(kernel, groups), out_shape=pltpu.VMEM(en...  50 us

profile of v1, /device:TPU:0, one launch (start us, length us, event | category | flops | bytes accessed | tf_op | source)
XLA Modules:
  0.0 51.0 jit_solution(12878533283452338529)
XLA Ops:
  0.0 50.0 %letkf.1 = bf16[16,32768]{1,0:T(8,128)(2,1)S(1)} custom-call(bf16[16,32768]{1,0:T(8,128)(2,1)} %ens_hbm.1, s32[8,256]{1,0:T(8,128)} %bitcast.3, s32[1,8]{1,0:T(1,128)} %count_hbm.1, f32[8,256]{1,0:T(8,128)} %bitcast.4, f32[8,256]{1,0:T(8,128)} %bitcast.5), custom_call_target="tpu_custom_call" | custom-call | tf_op jit(solution)/shard_map/letkf/pallas_call | solution.py:283
  50.0 1.0 %copy.7 = bf16[16,32768]{1,0:T(8,128)(2,1)} copy(bf16[16,32768]{1,0:T(8,128)(2,1)S(1)} %letkf.1) | data formatting | bytes 2097152

commit v2 on v1

--- a/solution.py
+++ b/solution.py
@@ -14,8 +14,9 @@
 inflation = 1.1
 
 MESH = pl.DeviceIdType.MESH
-CHUNK = 1
 HELD_BACK = 2
+EARLY_INNER = 4
+EARLY_OUTER = 3
 F32 = jnp.float32
 BF16 = jnp.bfloat16
 
@@ -123,6 +124,10 @@
     ret_recv,
     halo_send,
     halo_recv,
+    joined,
+    told,
+    spread,
+    complete,
 ):
     me = lax.axis_index("mem")
     blocks, _, width = arrived.shape
@@ -130,11 +135,43 @@
     slots = cell.shape[1]
     size = groups * local
 
+    lanes = 2
+    spots = groups // lanes
+    split = groups > 2 * lanes and groups % (2 * lanes) == 0
+
+    def central(peer):
+        spot = peer // lanes
+        return (spot == spots // 2 - 1) | (spot == spots // 2)
+
+    def notify(semaphore, peer):
+        pl.semaphore_signal(semaphore, inc=1, device_id={"mem": peer}, device_id_type=MESH)
+
+    others = [lax.rem(me + step, groups) for step in range(1, groups)]
     barrier = pltpu.get_barrier_semaphore()
-    for step in range(1, groups):
-        pl.semaphore_signal(
-            barrier, inc=1, device_id={"mem": lax.rem(me + step, groups)}, device_id_type=MESH
-        )
+    if split:
+        inner = central(me)
+        outer = jnp.logical_not(inner)
+        upper = me // lanes >= spots // 2
+        lane = lax.rem(me, lanes)
+        parent = (spots // 2 - 1 + upper.astype(jnp.int32)) * lanes + lane
+        first = jnp.where(upper, spots // 2 + 1, 0) * lanes + lane
+        children = [first + i * lanes for i in range(spots // 2 - 1)]
+
+        def to_central(semaphore):
+            for peer in others:
+                pl.when(central(peer))(lambda: notify(semaphore, peer))
+
+        def to_children(semaphore):
+            for child in children:
+                notify(semaphore, child)
+
+        @pl.when(inner)
+        def _():
+            to_central(barrier)
+            to_children(barrier)
+    else:
+        for peer in others:
+            notify(barrier, peer)
 
     loads = [
         pltpu.make_async_copy(source, target, load_sem.at[i])
@@ -144,7 +181,10 @@
     ]
     for load in loads:
         load.start()
-    pl.semaphore_wait(barrier, groups - 1)
+    if split:
+        pl.semaphore_wait(barrier, jnp.where(inner, 2 * lanes - 1, 1))
+    else:
+        pl.semaphore_wait(barrier, groups - 1)
 
     def columns(owner, b):
         start = pl.multiple_of((owner * blocks + b) * width, width)
@@ -154,18 +194,53 @@
         return pl.ds(pl.multiple_of(owner * local, local), local)
 
     order = [blocks - 1, *range(blocks - 1)]
-    for first in range(0, blocks, CHUNK):
-        for step in range(1, groups):
-            peer = lax.rem(me + step, groups)
-            for b in order[first : first + CHUNK]:
-                pltpu.make_async_remote_copy(
-                    src_ref=ens_hbm.at[:, columns(peer, b)],
-                    dst_ref=arrived.at[b, members_of(me), :],
-                    send_sem=fwd_send,
-                    recv_sem=fwd_recv.at[b],
-                    device_id={"mem": peer},
-                    device_id_type=MESH,
-                ).start()
+    def send_to(b, peer):
+        pltpu.make_async_remote_copy(
+            src_ref=ens_hbm.at[:, columns(peer, b)],
+            dst_ref=arrived.at[b, members_of(me), :],
+            send_sem=fwd_send,
+            recv_sem=fwd_recv.at[b],
+            device_id={"mem": peer},
+            device_id_type=MESH,
+        ).start()
+
+    def send_where(wanted, chosen):
+        for b in chosen:
+            for peer in others:
+                pl.when(wanted(peer))(lambda: send_to(b, peer))
+
+    def send_all(chosen):
+        for b in chosen:
+            for peer in others:
+                send_to(b, peer)
+
+    def beyond(peer):
+        return jnp.logical_not(central(peer))
+
+    if split:
+
+        @pl.when(inner)
+        def _():
+            send_where(central, order[:EARLY_INNER])
+            pl.semaphore_wait(joined, len(children))
+            to_children(told)
+            to_central(spread)
+            pl.semaphore_wait(spread, 2 * lanes - 1)
+            to_children(complete)
+            send_where(beyond, order[:EARLY_INNER])
+            send_all(order[EARLY_INNER:])
+
+        @pl.when(outer)
+        def _():
+            notify(joined, parent)
+            pl.semaphore_wait(told, 1)
+            send_where(central, order[:EARLY_OUTER])
+            pl.semaphore_wait(complete, 1)
+            send_where(beyond, order[:EARLY_OUTER])
+            send_all(order[EARLY_OUTER:])
+    else:
+        send_all(order)
+
     for b in order:
         pltpu.make_async_copy(
             ens_hbm.at[:, columns(me, b)], arrived.at[b, members_of(me), :], fwd_recv.at[b]
@@ -306,7 +381,8 @@
             pltpu.SemaphoreType.DMA,
             pltpu.SemaphoreType.DMA((2,)),
             pltpu.SemaphoreType.DMA((2,)),
-        ],
+        ]
+        + [pltpu.SemaphoreType.REGULAR] * 4,
         compiler_params=pltpu.CompilerParams(collective_id=0, has_side_effects=True),
         name="letkf",
     )(ensemble, obs_cell[0], obs_count, obs_value[0], obs_rinv[0])

time: 51.7 us -> 50.7 us (0.981)
  Pallas kernels: 50 us -> 49 us
    pallas_call x1, Pallas kernels: 50 us -> 49 us  [fused(): pl.pallas_call(functools.partial(kernel, groups), out_shape=pltpu.VMEM(en...]
where the time goes in v2:
time: 50.7 us; the launch traced here: 50 us
  Pallas kernels  49 us (97%)
  local copies, waits for them, and re-layouts  0.97 us (2%)
    pallas_call x1, Pallas kernels, fused(): pl.pallas_call(functools.partial(kernel, groups), out_shape=pltpu.VMEM(en...  49 us

profile of v2, /device:TPU:0, one launch (start us, length us, event | category | flops | bytes accessed | tf_op | source)
XLA Modules:
  0.0 50.0 jit_solution(15907075286189099753)
XLA Ops:
  0.0 49.0 %letkf.1 = bf16[16,32768]{1,0:T(8,128)(2,1)S(1)} custom-call(bf16[16,32768]{1,0:T(8,128)(2,1)} %ens_hbm.1, s32[8,256]{1,0:T(8,128)} %bitcast.3, s32[1,8]{1,0:T(1,128)} %count_hbm.1, f32[8,256]{1,0:T(8,128)} %bitcast.4, f32[8,256]{1,0:T(8,128)} %bitcast.5), custom_call_target="tpu_custom_call" | custom-call | tf_op jit(solution)/shard_map/letkf/pallas_call | solution.py:358
  49.0 1.0 %copy.7 = bf16[16,32768]{1,0:T(8,128)(2,1)} copy(bf16[16,32768]{1,0:T(8,128)(2,1)S(1)} %letkf.1) | data formatting | bytes 2097152

commit v3 on v2

--- a/solution.py
+++ b/solution.py
@@ -96,6 +96,37 @@
     return results
 
 
+def fold(gram):
+    size = gram.shape[1]
+    half = size // 2
+    top, bottom = gram[:half], pltpu.roll(gram[half:size], half, 1)
+    row = lax.broadcasted_iota(jnp.int32, top.shape, 0)
+    column = lax.broadcasted_iota(jnp.int32, top.shape, 1)
+    left = column < half
+    packed = jnp.where(left & (row > column), bottom, top)
+    diagonal = jnp.sum(jnp.where(left & (row == column), bottom, 0.0), axis=0, keepdims=True)
+    rest = gram[size:]
+    place = lax.broadcasted_iota(jnp.int32, rest.shape, 0)
+    rest = jnp.where(place == 1, jnp.broadcast_to(diagonal, rest.shape), rest)
+    return jnp.concatenate([packed, rest], axis=0).astype(BF16)
+
+
+def unfold(folded):
+    size = folded.shape[1]
+    half = size // 2
+    packed, rest = folded[:half].astype(F32), folded[half:].astype(F32)
+    turned = jnp.transpose(jnp.concatenate([packed, jnp.zeros_like(packed)], axis=0))
+    row = lax.broadcasted_iota(jnp.int32, packed.shape, 0)
+    column = lax.broadcasted_iota(jnp.int32, packed.shape, 1)
+    top = jnp.where((column < half) & (row > column), turned[:half], packed)
+    diagonal = jnp.broadcast_to(pltpu.roll(rest, half, 1)[1:2], packed.shape)
+    lower, upper = pltpu.roll(packed, half, 1), pltpu.roll(turned[:half], half, 1)
+    behind = column - half
+    corner = jnp.where(row > behind, lower, jnp.where(row < behind, upper, diagonal))
+    bottom = jnp.where(column < half, turned[half:], corner)
+    return jnp.concatenate([top, bottom, rest], axis=0)
+
+
 def kernel(
     groups,
     ens_hbm,
@@ -289,7 +320,7 @@
             ).start()
 
     def halo(slot, peer, which):
-        edge[which] = gram[slot].astype(BF16)
+        edge[which] = fold(gram[slot])
         return pltpu.make_async_remote_copy(
             src_ref=edge.at[which],
             dst_ref=far_edge.at[which],
@@ -322,9 +353,9 @@
         @pl.when(turn == pairs - 1)
         def _():
             upward.wait_recv()
-            gram[0] = far_edge[0].astype(F32)
+            gram[0] = unfold(far_edge[0])
             downward.wait_recv()
-            gram[blocks + 1] = far_edge[1].astype(F32)
+            gram[blocks + 1] = unfold(far_edge[1])
 
         final = turn == pairs - 1
         solve([jnp.where(final, 0, b), jnp.where(final, blocks - 1, b + 1)])
@@ -364,8 +395,8 @@
             pltpu.VMEM((blocks, size, width), BF16),
             pltpu.VMEM((blocks, size + 16, slots), BF16),
             pltpu.VMEM((blocks + 2, size + 16, size), F32),
-            pltpu.VMEM((2, size + 16, size), BF16),
-            pltpu.VMEM((2, size + 16, size), BF16),
+            pltpu.VMEM((2, size // 2 + 16, size), BF16),
+            pltpu.VMEM((2, size // 2 + 16, size), BF16),
             pltpu.VMEM((blocks, width, slots), BF16),
             pltpu.VMEM((blocks, size, width), BF16),
             pltpu.VMEM((blocks, slots), F32),

time: 50.7 us -> 50.4 us (level)
  no operation moved by 1% of the time
where the time goes in v3:
time: 50.4 us; the launch traced here: 49.7 us
  Pallas kernels  48.7 us (97%)
  local copies, waits for them, and re-layouts  0.97 us (2%)
    pallas_call x1, Pallas kernels, fused(): pl.pallas_call(functools.partial(kernel, groups), out_shape=pltpu.VMEM(en...  48.7 us

profile of v3, /device:TPU:0, one launch (start us, length us, event | category | flops | bytes accessed | tf_op | source)
XLA Modules:
  0.0 49.7 jit_solution(11176751486817284803)
XLA Ops:
  0.0 48.7 %letkf.1 = bf16[16,32768]{1,0:T(8,128)(2,1)S(1)} custom-call(bf16[16,32768]{1,0:T(8,128)(2,1)} %ens_hbm.1, s32[8,256]{1,0:T(8,128)} %bitcast.3, s32[1,8]{1,0:T(1,128)} %count_hbm.1, f32[8,256]{1,0:T(8,128)} %bitcast.4, f32[8,256]{1,0:T(8,128)} %bitcast.5), custom_call_target="tpu_custom_call" | custom-call | tf_op jit(solution)/shard_map/letkf/pallas_call | solution.py:389
  48.7 1.0 %copy.7 = bf16[16,32768]{1,0:T(8,128)(2,1)} copy(bf16[16,32768]{1,0:T(8,128)(2,1)S(1)} %letkf.1) | data formatting | bytes 2097152

commit v4 on v3

--- a/solution.py
+++ b/solution.py
@@ -168,7 +168,7 @@
 
     lanes = 2
     spots = groups // lanes
-    split = groups > 2 * lanes and groups % (2 * lanes) == 0
+    split = groups == 4 * lanes
 
     def central(peer):
         spot = peer // lanes
@@ -182,19 +182,24 @@
     if split:
         inner = central(me)
         outer = jnp.logical_not(inner)
-        upper = me // lanes >= spots // 2
-        lane = lax.rem(me, lanes)
-        parent = (spots // 2 - 1 + upper.astype(jnp.int32)) * lanes + lane
-        first = jnp.where(upper, spots // 2 + 1, 0) * lanes + lane
-        children = [first + i * lanes for i in range(spots // 2 - 1)]
+        spot, lane = me // lanes, lax.rem(me, lanes)
+        upper = spot >= spots // 2
+        turn_lane = 1 - 2 * lane
+        across = (spots - 1 - spot) * lanes + lane
+        slant, beside = across + turn_lane, me + turn_lane
+        parent = jnp.where(upper, spots // 2, spots // 2 - 1) * lanes + lane
+        child = jnp.where(upper, spots - 1, 0) * lanes + lane
+        opposite = jnp.where(upper, spots // 2 - 1, spots // 2) * lanes + lane
+        near_mid = [parent, parent + turn_lane]
+        far_mid = [opposite, opposite + turn_lane]
+        middle = (across, beside, slant)
 
         def to_central(semaphore):
-            for peer in others:
-                pl.when(central(peer))(lambda: notify(semaphore, peer))
+            for peer in middle:
+                notify(semaphore, peer)
 
         def to_children(semaphore):
-            for child in children:
-                notify(semaphore, child)
+            notify(semaphore, child)
 
         @pl.when(inner)
         def _():
@@ -240,6 +245,11 @@
             for peer in others:
                 pl.when(wanted(peer))(lambda: send_to(b, peer))
 
+    def send_to_some(peers, chosen):
+        for b in chosen:
+            for peer in peers:
+                send_to(b, peer)
+
     def send_all(chosen):
         for b in chosen:
             for peer in others:
@@ -252,8 +262,8 @@
 
         @pl.when(inner)
         def _():
-            send_where(central, order[:EARLY_INNER])
-            pl.semaphore_wait(joined, len(children))
+            send_to_some(middle, order[:EARLY_INNER])
+            pl.semaphore_wait(joined, 1)
             to_children(told)
             to_central(spread)
             pl.semaphore_wait(spread, 2 * lanes - 1)
@@ -265,9 +275,9 @@
         def _():
             notify(joined, parent)
             pl.semaphore_wait(told, 1)
-            send_where(central, order[:EARLY_OUTER])
+            send_to_some(far_mid + near_mid, order[:EARLY_OUTER])
             pl.semaphore_wait(complete, 1)
-            send_where(beyond, order[:EARLY_OUTER])
+            send_to_some((beside, across, slant), order[:EARLY_OUTER])
             send_all(order[EARLY_OUTER:])
     else:
         send_all(order)

time: 50.4 us -> 50.4 us (level)
  no operation moved by 1% of the time
where the time goes in v4:
time: 50.4 us; the launch traced here: 49.7 us
  Pallas kernels  48.7 us (97%)
  local copies, waits for them, and re-layouts  0.97 us (2%)
    pallas_call x1, Pallas kernels, fused(): pl.pallas_call(functools.partial(kernel, groups), out_shape=pltpu.VMEM(en...  48.7 us

profile of v4, /device:TPU:0, one launch (start us, length us, event | category | flops | bytes accessed | tf_op | source)
XLA Modules:
  0.0 49.7 jit_solution(11335172457550213318)
XLA Ops:
  0.0 48.7 %letkf.1 = bf16[16,32768]{1,0:T(8,128)(2,1)S(1)} custom-call(bf16[16,32768]{1,0:T(8,128)(2,1)} %ens_hbm.1, s32[8,256]{1,0:T(8,128)} %bitcast.3, s32[1,8]{1,0:T(1,128)} %count_hbm.1, f32[8,256]{1,0:T(8,128)} %bitcast.4, f32[8,256]{1,0:T(8,128)} %bitcast.5), custom_call_target="tpu_custom_call" | custom-call | tf_op jit(solution)/shard_map/letkf/pallas_call | solution.py:399
  48.7 1.0 %copy.7 = bf16[16,32768]{1,0:T(8,128)(2,1)} copy(bf16[16,32768]{1,0:T(8,128)(2,1)S(1)} %letkf.1) | data formatting | bytes 2097152

commit v5 on v4

--- a/solution.py
+++ b/solution.py
@@ -161,6 +161,7 @@
     complete,
 ):
     me = lax.axis_index("mem")
+    odd = lax.rem(lax.axis_index("blk"), 2) == 1
     blocks, _, width = arrived.shape
     local = ens_hbm.shape[0]
     slots = cell.shape[1]
@@ -269,7 +270,7 @@
             pl.semaphore_wait(spread, 2 * lanes - 1)
             to_children(complete)
             send_where(beyond, order[:EARLY_INNER])
-            send_all(order[EARLY_INNER:])
+            send_all(order[EARLY_INNER:6])
 
         @pl.when(outer)
         def _():
@@ -278,9 +279,13 @@
             send_to_some(far_mid + near_mid, order[:EARLY_OUTER])
             pl.semaphore_wait(complete, 1)
             send_to_some((beside, across, slant), order[:EARLY_OUTER])
-            send_all(order[EARLY_OUTER:])
+            send_all(order[EARLY_OUTER:6])
     else:
-        send_all(order)
+        send_all(order[:6])
+
+    @pl.when(jnp.logical_not(odd))
+    def _():
+        send_all(order[6:])
 
     for b in order:
         pltpu.make_async_copy(
@@ -341,6 +346,11 @@
         )
 
     take_block(blocks - 1)
+
+    @pl.when(odd)
+    def _():
+        send_all(order[6:])
+
     upward = halo(blocks, lax.rem(me + 1, groups), 0)
     upward.start()
     take_block(0)

time: 50.4 us -> 50.4 us (level)
  no operation moved by 1% of the time
where the time goes in v5:
time: 50.4 us; the launch traced here: 49.7 us
  Pallas kernels  48.7 us (97%)
  local copies, waits for them, and re-layouts  0.97 us (2%)
    pallas_call x1, Pallas kernels, fused(): pl.pallas_call(functools.partial(kernel, groups), out_shape=pltpu.VMEM(en...  48.7 us

profile of v5, /device:TPU:0, one launch (start us, length us, event | category | flops | bytes accessed | tf_op | source)
XLA Modules:
  0.0 49.7 jit_solution(15514587048069667024)
XLA Ops:
  0.0 48.7 %letkf.1 = bf16[16,32768]{1,0:T(8,128)(2,1)S(1)} custom-call(bf16[16,32768]{1,0:T(8,128)(2,1)} %ens_hbm.1, s32[8,256]{1,0:T(8,128)} %bitcast.3, s32[1,8]{1,0:T(1,128)} %count_hbm.1, f32[8,256]{1,0:T(8,128)} %bitcast.4, f32[8,256]{1,0:T(8,128)} %bitcast.5), custom_call_target="tpu_custom_call" | custom-call | tf_op jit(solution)/shard_map/letkf/pallas_call | solution.py:409
  48.7 1.0 %copy.7 = bf16[16,32768]{1,0:T(8,128)(2,1)} copy(bf16[16,32768]{1,0:T(8,128)(2,1)S(1)} %letkf.1) | data formatting | bytes 2097152
